TPU v7x, 32 devices: a whole 2x2x4 slice. The times are simulated.
32 devices in a mesh: frame: 8 (over z, y), head: 4 (over x, core).
Axes of the slice: x: 2, y: 2, z: 4, core: 2. Of those that a mesh axis runs over, the one named last changes fastest.
Arguments:
- latents: bfloat16 [4096, 5120], P('frame', 'head'), may hold values from -6 to 6
- queries: bfloat16 [4096, 2560], P('frame', 'head'), may hold values from -22 to 22
- keys: bfloat16 [4096, 2560], P('frame', 'head'), may hold values from -6 to 6
- values: bfloat16 [4096, 2560], P('frame', 'head'), may hold values from -6 to 6
- out_weight: bfloat16 [2560, 5120], P('head'), may hold values from -0.5 to 0.5
- gate_table: float32 [4, 5120], P(None, 'head'), may hold values from 0.5 to 2
- levels: int32 [8], P('frame'), may hold values from 0 to 3
- block_mask: int32 [8, 4], P('frame'), may hold values from 0 to 1, as said below
- fresh: bfloat16 [512, 5120], P(None, 'head'), may hold values from -6 to 6
Outputs:
- velocity: bfloat16 [4096, 5120], P('frame', 'head')
- next_latents: bfloat16 [4096, 5120], P('frame', 'head')
Inputs may be any that keep to these rules, and one draw needn't show every extreme that they name: block_mask[c, 0] is 1 for every span c.
All inputs are finite; a program needn't handle non-finite values.
Results may differ from a plain program's by a relative error of at most 0.012.
Values may be sent and summed in bfloat16 or wider, within the bound.
A program may use at most 128 MiB of HBM per device.

v0:
```python
import functools
import math

import jax
import jax.numpy as jnp
from jax import lax
from jax.experimental import pallas as pl
from jax.experimental.pallas import tpu as pltpu
from jax.sharding import PartitionSpec as P

HD = 128
LANES = 128
LEVELS = 4
FAR = 1e30
LOW = -1e20

flow_shift = 5.0

MESH = pl.DeviceIdType.MESH
bf16 = jnp.bfloat16
f32 = jnp.float32


def noise_level(point):
    return flow_shift * point / (1.0 + (flow_shift - 1.0) * point)


def partial_attention(query, blocks, penalties):
    scale = math.log2(math.e) / math.sqrt(HD)
    scores = [
        lax.dot_general(query, k, (((1,), (1,)), ((), ())), preferred_element_type=f32) * scale
        for k, _ in blocks
    ]
    top = LOW
    for s, penalty in zip(scores, penalties):
        top = jnp.maximum(top, jnp.max(s, axis=1, keepdims=True) - penalty)
    acc = 0.0
    for s, penalty, (_, v) in zip(scores, penalties, blocks):
        weights = jnp.exp2(s - (top + penalty)).astype(bf16)
        wide = jnp.concatenate([v, jnp.ones((v.shape[0], LANES), bf16)], axis=1)
        acc = acc + jnp.dot(weights, wide, preferred_element_type=f32)
    total = jnp.maximum(acc[:, HD:], 1.0)
    return acc[:, :HD] / total, top + jnp.log2(total)


def kernel(
    levels_ref, mask_ref, q_hbm, k_hbm, v_hbm, w_hbm, lat_hbm, fresh_hbm, gate_ref,
    vel_hbm, next_hbm,
    q_own, k_own, v_own, q_guest, k_prev, v_prev, pen_own, pen_guest,
    o_send, o_recv, st_send, st_recv, o_loc, lse_loc, attended, w_ref, lat_ref, gate_row,
    pair_send, pair_recv, near_send, near_recv, far_send, far_recv, vel_stage, upd_stage,
    in_sem, bulk_sem, kv_ss, kv_rs, q_ss, q_rs, o_ss, o_rs, st_ss, st_rs, pen_sem,
    pair_ss, pair_rs, near_ss, near_rs, far_ss, far_rs, vel_sem, slide_ss, slide_rs,
):
    f = lax.axis_index("frame")
    frames = lax.axis_size("frame")
    me = lax.axis_index("head")
    heads, span, _ = q_own.shape
    pieces, prow, pcol = pair_send.shape
    row_parts = span // prow
    out_width = lat_ref.shape[1]
    tile = min(span, 256)

    pair = me + 1 - 2 * (me % 2)
    far = (me + 2) % 4
    has_prev = f >= 1
    has_down = f >= 2
    has_next = f + 1 < frames
    has_up = f + 2 < frames

    def remote(src, dst, ss, rs, frame=None, head=None):
        where = {"frame": frame} if head is None else {"head": head}
        return pltpu.make_async_remote_copy(
            src_ref=src, dst_ref=dst, send_sem=ss, recv_sem=rs, device_id=where, device_id_type=MESH
        )

    def columns(h):
        return pl.ds(pl.multiple_of(h * HD, HD), HD)

    def local_in(h):
        return [
            pltpu.make_async_copy(src.at[:, columns(h)], dst.at[h], in_sem.at[h, i])
            for i, (src, dst) in enumerate(((k_hbm, k_own), (q_hbm, q_own), (v_hbm, v_own)))
        ]

    w_in = pltpu.make_async_copy(w_hbm, w_ref, bulk_sem.at[0])
    lat_in = pltpu.make_async_copy(lat_hbm, lat_ref, bulk_sem.at[1])

    def k_copy(h):
        return remote(k_hbm.at[:, columns(h)], k_prev.at[h], kv_ss.at[h, 0], kv_rs.at[h, 0], frame=f + 1)

    def v_copy(h):
        return remote(v_hbm.at[:, columns(h)], v_prev.at[h], kv_ss.at[h, 1], kv_rs.at[h, 1], frame=f + 1)

    def q_copy(h):
        return remote(q_hbm.at[:, columns(h)], q_guest.at[h], q_ss.at[h], q_rs.at[h], frame=f - 2)

    def o_copy(h):
        return remote(o_send.at[h], o_recv.at[h], o_ss.at[h], o_rs.at[h], frame=f + 2)

    def st_copy(h):
        return remote(st_send.at[h], st_recv.at[h], st_ss.at[h], st_rs.at[h], frame=f + 2)

    pen_copy = remote(pen_own, pen_guest, pen_sem.at[0], pen_sem.at[1], frame=f - 2)

    barrier = pltpu.get_barrier_semaphore()
    for there, step in ((has_prev, -1), (has_down, -2), (has_next, 1), (has_up, 2)):
        @pl.when(there)
        def _():
            pl.semaphore_signal(barrier, inc=1, device_id={"frame": f + step}, device_id_type=MESH)
    for peer in (pair, far):
        pl.semaphore_signal(barrier, inc=1, device_id={"head": peer}, device_id_type=MESH)

    for h in range(heads):
        for copy in local_in(h):
            copy.start()
    w_in.start()
    lat_in.start()

    for k in range(4):
        allowed = (mask_ref[0, k] == 1) & (f - k >= 0)
        pen_own[k:k + 1, :] = jnp.full((1, LANES), jnp.where(allowed, 0.0, FAR), f32)
    pen_own[4:, :] = jnp.zeros((4, LANES), f32)

    @pl.when(f == 0)
    def _():
        k_prev[...] = jnp.zeros_like(k_prev)
        v_prev[...] = jnp.zeros_like(v_prev)

    @pl.when(f < 2)
    def _():
        o_recv[...] = jnp.zeros_like(o_recv)
        st_recv[...] = jnp.full(st_recv.shape, LOW, f32)

    others = (
        2 + has_prev.astype(jnp.int32) + has_down.astype(jnp.int32)
        + has_next.astype(jnp.int32) + has_up.astype(jnp.int32)
    )
    pl.semaphore_wait(barrier, others)

    @pl.when(has_down)
    def _():
        pen_copy.start()
    for h in range(heads):
        @pl.when(has_next)
        def _():
            k_copy(h).start()
            v_copy(h).start()

        @pl.when(has_down)
        def _():
            q_copy(h).start()

    eye = lax.broadcasted_iota(jnp.int32, (LANES, LANES), 0) == lax.broadcasted_iota(
        jnp.int32, (LANES, LANES), 1
    )

    @pl.when(has_up)
    def _():
        pen_copy.wait_recv()

    def merge(h):
        @pl.when(has_down)
        def _():
            o_copy(h).wait_recv()
            st_copy(h).wait_recv()
        for a in range(span // LANES):
            rows = pl.ds(a * LANES, LANES)
            guest_lse = jnp.sum(
                jnp.where(eye, st_recv[h, a:a + 1, :], 0.0), axis=1, keepdims=True
            )
            share = 1.0 / (1.0 + jnp.exp2(lse_loc[h, rows, :] - guest_lse))
            mine = o_loc[h, rows, :]
            both = mine + share * (o_recv[h, rows, :].astype(f32) - mine)
            attended[rows, columns(h)] = both.astype(bf16)

    def one_head(h, carry):
        for copy in local_in(h):
            copy.wait()

        @pl.when(has_prev)
        def _():
            k_copy(h).wait_recv()
            v_copy(h).wait_recv()
        blocks = ((k_own[h], v_own[h]), (k_prev[h], v_prev[h]))

        @pl.when(has_up)
        def _():
            q_copy(h).wait_recv()
            for t in range(span // tile):
                rows = pl.ds(t * tile, tile)
                out, lse = partial_attention(
                    q_guest[h, rows, :], blocks, (pen_guest[2:3, 0:1], pen_guest[3:4, 0:1])
                )
                o_send[h, rows, :] = out.astype(bf16)
                for a in range(tile // LANES):
                    at = t * (tile // LANES) + a
                    st_send[h, at:at + 1, :] = jnp.sum(
                        jnp.where(eye, lse[a * LANES:(a + 1) * LANES, :], 0.0), axis=0, keepdims=True
                    )
            o_copy(h).start()
            st_copy(h).start()

        for t in range(span // tile):
            rows = pl.ds(t * tile, tile)
            out, lse = partial_attention(
                q_own[h, rows, :], blocks, (pen_own[0:1, 0:1], pen_own[1:2, 0:1])
            )
            o_loc[h, rows, :] = out
            lse_loc[h, rows, :] = lse

        @pl.when(h >= 1)
        def _():
            merge(h - 1)
        return carry

    lax.fori_loop(0, heads, one_head, 0)
    merge(heads - 1)

    w_in.wait()
    lat_in.wait()
    level = jnp.full((1, LANES), levels_ref[0], jnp.int32).astype(f32)
    delta = (noise_level(level / LEVELS) - noise_level((level + 1.0) / LEVELS))[:, 0:1]
    gate = jnp.zeros((1, out_width), f32)
    for n in range(LEVELS):
        gate = gate + jnp.where(level[:, 0:1] == float(n), gate_ref[n:n + 1, :], 0.0)
    gate_row[...] = gate

    def at_rows(i):
        return pl.ds(pl.multiple_of((i % row_parts) * prow, prow), prow)

    def at_cols(i, base=0):
        return pl.ds(pl.multiple_of(base + (i // row_parts) * pcol, LANES), pcol)

    def project(i, owner):
        return jnp.dot(
            attended[at_rows(i), :], w_ref[:, at_cols(i, owner * out_width)],
            preferred_element_type=f32,
        )

    def pair_copy(i):
        return remote(pair_send.at[i], pair_recv.at[i], pair_ss.at[i], pair_rs.at[i], head=pair)

    def near_copy(i):
        return remote(near_send.at[i], near_recv.at[i], near_ss.at[i], near_rs.at[i], head=pair)

    def far_copy(i):
        return remote(far_send.at[i], far_recv.at[i], far_ss.at[i], far_rs.at[i], head=far)

    def slide_copy(i):
        return remote(
            upd_stage.at[i], next_hbm.at[at_rows(i), at_cols(i)], slide_ss.at[i], slide_rs.at[i],
            frame=f - 1,
        )

    def vel_copy(i):
        return pltpu.make_async_copy(
            vel_stage.at[i], vel_hbm.at[at_rows(i), at_cols(i)], vel_sem.at[i]
        )

    diagonal = (pair + 2) % 4

    def send_pair(i):
        pair_send[i] = project(i, diagonal).astype(bf16)
        pair_copy(i).start()

    send_pair(0)

    def exchange(i, carry):
        @pl.when(i + 1 < pieces)
        def _():
            send_pair(i + 1)
        mine = project(i, far)
        pair_copy(i).wait_recv()
        far_send[i] = (mine.astype(bf16).astype(f32) + pair_recv[i].astype(f32)).astype(bf16)
        far_copy(i).start()
        return carry

    lax.fori_loop(0, pieces, exchange, 0)

    def send_near(i, carry):
        near_send[i] = project(i, pair).astype(bf16)
        near_copy(i).start()
        return carry

    lax.fori_loop(0, pieces, send_near, 0)

    def join(i, carry):
        total = project(i, me).astype(bf16).astype(f32)
        near_copy(i).wait_recv()
        far_copy(i).wait_recv()
        total = total + near_recv[i].astype(f32) + far_recv[i].astype(f32)
        gated = gate_row[0:1, at_cols(i)] * total
        upd_stage[i] = (lat_ref[at_rows(i), at_cols(i)].astype(f32) + delta * gated).astype(bf16)

        @pl.when(has_prev)
        def _():
            slide_copy(i).start()
        vel_stage[i] = gated.astype(bf16)
        vel_copy(i).start()
        return carry

    lax.fori_loop(0, pieces, join, 0)

    for h in range(heads):
        @pl.when(has_next)
        def _():
            k_copy(h).wait_send()
            v_copy(h).wait_send()

        @pl.when(has_down)
        def _():
            q_copy(h).wait_send()

        @pl.when(has_up)
        def _():
            o_copy(h).wait_send()
            st_copy(h).wait_send()

    @pl.when(has_down)
    def _():
        pen_copy.wait_send()

    @pl.when(f == frames - 1)
    def _():
        fresh_in = pltpu.make_async_copy(fresh_hbm, lat_ref, bulk_sem.at[0])
        fresh_in.start()
        fresh_in.wait()
        fresh_out = pltpu.make_async_copy(lat_ref, next_hbm, bulk_sem.at[1])
        fresh_out.start()
        fresh_out.wait()

    def drain(i, carry):
        pair_copy(i).wait_send()
        near_copy(i).wait_send()
        far_copy(i).wait_send()
        vel_copy(i).wait()

        @pl.when(has_prev)
        def _():
            slide_copy(i).wait_send()

        @pl.when(has_next)
        def _():
            slide_copy(i).wait_recv()
        return carry

    lax.fori_loop(0, pieces, drain, 0)


def shards(latents, queries, keys, values, out_weight, gate_table, levels, block_mask, fresh):
    span, hh = queries.shape
    heads = hh // HD
    out_width = latents.shape[1]
    assert lax.axis_size("head") == 4 and block_mask.shape[1] == 4
    assert out_weight.shape[1] == 4 * out_width
    prow = span // 2
    pcol = 2 * LANES if out_width % (2 * LANES) == 0 else LANES
    pieces = (span // prow) * (out_width // pcol)

    vmem = pltpu.VMEM
    dma = pltpu.SemaphoreType.DMA
    head_block = vmem((heads, span, HD), bf16)
    head_wide = vmem((heads, span, HD), f32)
    stats = vmem((heads, 8, LANES), f32)
    piece = vmem((pieces, prow, pcol), bf16)
    any_spec = pl.BlockSpec(memory_space=pl.ANY)
    out = jax.ShapeDtypeStruct((span, out_width), bf16)
    return pl.pallas_call(
        kernel,
        in_specs=[pl.BlockSpec(memory_space=pltpu.SMEM)] * 2 + [any_spec] * 6
        + [pl.BlockSpec(memory_space=pltpu.VMEM)],
        out_specs=[any_spec, any_spec],
        out_shape=[out, out],
        scratch_shapes=[head_block] * 6
        + [vmem((8, LANES), f32)] * 2
        + [head_block, head_block, stats, stats, head_wide, head_wide]
        + [vmem((span, hh), bf16), vmem(out_weight.shape, bf16), vmem((span, out_width), bf16)]
        + [vmem((1, out_width), f32)]
        + [piece] * 8
        + [dma((heads, 3)), dma((2,)), dma((heads, 2)), dma((heads, 2))]
        + [dma((heads,))] * 6
        + [dma((2,))]
        + [dma((pieces,))] * 9,
        compiler_params=pltpu.CompilerParams(
            collective_id=0, has_side_effects=True, vmem_limit_bytes=60 * 1024 * 1024
        ),
    )(levels, block_mask, queries, keys, values, out_weight, latents, fresh, gate_table)


def solution(mesh):
    in_specs = (
        P("frame", "head"),
        P("frame", "head"),
        P("frame", "head"),
        P("frame", "head"),
        P("head", None),
        P(None, "head"),
        P("frame"),
        P("frame", None),
        P(None, "head"),
    )
    out_specs = (P("frame", "head"), P("frame", "head"))
    return jax.shard_map(shards, mesh=mesh, in_specs=in_specs, out_specs=out_specs, check_vma=False)
```

profile of v0, /device:TPU:25, one launch (start us, length us, event | category | flops | bytes accessed | tf_op | source)
XLA Modules:
  0.0 95.1 jit_solution(16183008520236961202)
XLA Ops:
  1.3 90.2 %shard_map.104 = (bf16[512,1280]{1,0:T(8,128)(2,1)}, bf16[512,1280]{1,0:T(8,128)(2,1)}) custom-call(s32[1]{0:T(128)S(6)} %copy.13.levels_ref, s32[1,4]{1,0:T(1,128)} %mask_ref.1, bf16[512,640]{1,0:T(8,128)(2,1)} %q_hbm.1, bf16[512,640]{1,0:T(8,128)(2,1)} %k_hbm.1, bf16[512,640]{1,0:T(8,128)(2,1)} %v_hbm.1, bf16[640,5120]{1,0:T(8,128)(2,1)} %w_hbm.1, ...), custom_call_target="tpu_custom_call" | custom-call | tf_op jit(solution)/shard_map/pallas_call | solution.py:369
  91.5 0.0 copy-start
  91.5 2.6 %copy.14 = bf16[512,1280]{1,0:T(8,128)(2,1)} copy(bf16[512,1280]{1,0:T(8,128)(2,1)} %get-tuple-element.4) | data formatting | bytes 2621440
  94.1 0.0 copy-done
  94.1 1.1 %copy.15 = bf16[512,1280]{1,0:T(8,128)(2,1)} copy(bf16[512,1280]{1,0:T(8,128)(2,1)S(1)} %copy-done) | data formatting | bytes 2621440
Async XLA Ops:
  91.5 2.6 %copy-start = (bf16[512,1280]{1,0:T(8,128)(2,1)S(1)}, bf16[512,1280]{1,0:T(8,128)(2,1)}, u32[]{:S(2)}) copy-start(bf16[512,1280]{1,0:T(8,128)(2,1)} %get-tuple-element.5) | copy-start | bytes 3932164
where the time goes:
time: 95.3 us; the launch traced here: 95.1 us
  Pallas kernels  90.2 us (95%)
  local copies, waits for them, and re-layouts  3.62 us (4%)
  between operations  1.3 us (1%)
    pallas_call x1, Pallas kernels, shards(): pl.pallas_call(kernel, in_specs=[pl.BlockSpec(memory_space=pltpu.SMEM)] *...  90.2 us
    unnamed x4, local copies, waits for them, and re-layouts  3.62 us

commit v1 on v0

v1 whole, which is shorter than its diff:
```python
import functools
import math

import jax
import jax.numpy as jnp
from jax import lax
from jax.experimental import pallas as pl
from jax.experimental.pallas import tpu as pltpu
from jax.sharding import PartitionSpec as P

HD = 128
LANES = 128
LEVELS = 4
FAR = 1e30
LOW = -1e20
VMEM_LIMIT = 60 * 1024 * 1024

flow_shift = 5.0

MESH = pl.DeviceIdType.MESH
bf16 = jnp.bfloat16
f32 = jnp.float32


def noise_level(point):
    return flow_shift * point / (1.0 + (flow_shift - 1.0) * point)


def scores_of(query, keys):
    scale = math.log2(math.e) / math.sqrt(HD)
    return lax.dot_general(query, keys, (((1,), (1,)), ((), ())), preferred_element_type=f32) * scale


def with_ones(values):
    return jnp.concatenate([values, jnp.ones((values.shape[0], LANES), bf16)], axis=1)


def kernel(
    levels_hbm, mask_hbm, q_hbm, k_hbm, v_hbm, w_hbm, lat_hbm, fresh_hbm, gate_hbm,
    vel_hbm, next_hbm,
    levels_ref, mask_ref, gate_ref,
    q_own, k_own, v_own, q_guest, k_prev, v_prev, v_relay, pen_own, pen_guest,
    acc_ref, top_ref, p_ref,
    o_send, o_recv, st_send, st_recv, o_loc, lse_loc, attended, w_ref, lat_ref, gate_row,
    pair_send, pair_recv, near_send, near_recv, far_send, far_recv, vel_stage, upd_stage,
    in_sem, bulk_sem, kv_ss, kv_rs, relay_ss, relay_rs, q_ss, q_rs, o_ss, o_rs, st_ss, st_rs, pen_sem,
    pair_ss, pair_rs, near_ss, near_rs, far_ss, far_rs, vel_sem, slide_ss, slide_rs,
):
    f = lax.axis_index("frame")
    frames = lax.axis_size("frame")
    me = lax.axis_index("head")
    heads, span, _ = q_own.shape
    pieces, prow, pcol = pair_send.shape
    row_parts = span // prow
    col_parts = pieces // row_parts
    out_width = lat_ref.shape[1]
    tile = prow
    tiles = span // tile
    lag = min(3, pieces)

    pair = me + 1 - 2 * (me % 2)
    far = (me + 2) % 4
    odd = f % 2 == 1
    even = f % 2 == 0
    has_prev = f >= 1
    has_down = f >= 2
    has_next = f + 1 < frames
    has_up = f + 2 < frames

    def remote(src, dst, ss, rs, frame=None, head=None):
        where = {"frame": frame} if head is None else {"head": head}
        return pltpu.make_async_remote_copy(
            src_ref=src, dst_ref=dst, send_sem=ss, recv_sem=rs, device_id=where, device_id_type=MESH
        )

    def columns(h):
        return pl.ds(pl.multiple_of(h * HD, HD), HD)

    def local_in(h):
        return [
            pltpu.make_async_copy(src.at[:, columns(h)], dst.at[h], in_sem.at[h, i])
            for i, (src, dst) in enumerate(((k_hbm, k_own), (q_hbm, q_own), (v_hbm, v_own)))
        ]

    w_in = pltpu.make_async_copy(w_hbm, w_ref, bulk_sem.at[0])
    lat_in = pltpu.make_async_copy(lat_hbm, lat_ref, bulk_sem.at[1])
    mask_in = pltpu.make_async_copy(mask_hbm, mask_ref, bulk_sem.at[2])
    levels_in = pltpu.make_async_copy(levels_hbm, levels_ref, bulk_sem.at[3])
    gate_in = pltpu.make_async_copy(gate_hbm, gate_ref, bulk_sem.at[4])

    def k_copy(h):
        return remote(k_hbm.at[:, columns(h)], k_prev.at[h], kv_ss.at[h, 0], kv_rs.at[h, 0], frame=f + 1)

    def v_copy(h):
        return remote(v_hbm.at[:, columns(h)], v_prev.at[h], kv_ss.at[h, 1], kv_rs.at[h, 1], frame=f + 1)

    def relay_in(h):
        return remote(
            v_hbm.at[:, columns(h)], v_relay.at[h], relay_ss.at[h], relay_rs.at[h], frame=f - 1
        )

    def relay_out(h):
        return remote(v_relay.at[h], v_prev.at[h], kv_ss.at[h, 1], kv_rs.at[h, 1], frame=f + 2)

    def q_copy(h):
        return remote(q_hbm.at[:, columns(h)], q_guest.at[h], q_ss.at[h], q_rs.at[h], frame=f - 2)

    def o_copy(h, t):
        rows = pl.ds(t * tile, tile)
        return remote(
            o_send.at[h, rows], o_recv.at[h, rows], o_ss.at[h, t], o_rs.at[h, t], frame=f + 2
        )

    def st_copy(h, t):
        return remote(st_send.at[h, t], st_recv.at[h, t], st_ss.at[h, t], st_rs.at[h, t], frame=f + 2)

    pen_copy = remote(pen_own, pen_guest, pen_sem.at[0], pen_sem.at[1], frame=f - 2)

    barrier = pltpu.get_barrier_semaphore()
    for there, step in ((has_prev, -1), (has_down, -2), (has_next, 1), (has_up, 2)):
        @pl.when(there)
        def _():
            pl.semaphore_signal(barrier, inc=1, device_id={"frame": f + step}, device_id_type=MESH)
    for peer in (pair, far):
        pl.semaphore_signal(barrier, inc=1, device_id={"head": peer}, device_id_type=MESH)

    mask_in.start()
    for h in range(heads):
        for copy in local_in(h):
            copy.start()

    @pl.when(f == 0)
    def _():
        k_prev[...] = jnp.zeros_like(k_prev)
        v_prev[...] = jnp.zeros_like(v_prev)

    @pl.when(f < 2)
    def _():
        o_recv[...] = jnp.zeros_like(o_recv)
        st_recv[...] = jnp.full(st_recv.shape, LOW, f32)

    @pl.when(f + 2 >= frames)
    def _():
        q_guest[...] = jnp.zeros_like(q_guest)
        pen_guest[...] = jnp.zeros_like(pen_guest)

    others = (
        2 + has_prev.astype(jnp.int32) + has_down.astype(jnp.int32)
        + has_next.astype(jnp.int32) + has_up.astype(jnp.int32)
    )
    pl.semaphore_wait(barrier, others)

    @pl.when(even & has_next)
    def _():
        for h in range(heads):
            k_copy(h).start()
            v_copy(h).start()

    @pl.when(odd & has_next)
    def _():
        for h in range(heads):
            relay_in(h).start()

    @pl.when(has_down)
    def _():
        for h in range(heads):
            q_copy(h).start()

    w_in.start()
    levels_in.start()
    gate_in.start()
    lat_in.start()

    mask_in.wait()
    for k in range(4):
        allowed = (mask_ref[0, k] == 1) & (f - k >= 0)
        pen_own[k:k + 1, :] = jnp.full((1, LANES), jnp.where(allowed, 0.0, FAR), f32)
    pen_own[4:, :] = jnp.zeros((4, LANES), f32)

    @pl.when(has_down)
    def _():
        pen_copy.start()

    @pl.when(odd & has_next)
    def _():
        relay_in(0).wait_send()
        for h in range(heads):
            k_copy(h).start()

    eye = lax.broadcasted_iota(jnp.int32, (LANES, LANES), 0) == lax.broadcasted_iota(
        jnp.int32, (LANES, LANES), 1
    )

    def merge(h, t):
        @pl.when(has_down)
        def _():
            o_copy(h, t).wait_recv()
            st_copy(h, t).wait_recv()
        for a in range(tile // LANES):
            rows = pl.ds(t * tile + a * LANES, LANES)
            guest_lse = jnp.sum(
                jnp.where(eye, st_recv[h, t, a:a + 1, :], 0.0), axis=1, keepdims=True
            )
            share = 1.0 / (1.0 + jnp.exp2(lse_loc[h, rows, :] - guest_lse))
            mine = o_loc[h, rows, :]
            both = mine + share * (o_recv[h, rows, :].astype(f32) - mine)
            attended[rows, columns(h)] = both.astype(bf16)

    @pl.when(has_up)
    def _():
        pen_copy.wait_recv()

    def forward(h):
        @pl.when(even & has_up)
        def _():
            relay_in(h).wait_recv()
            relay_out(h).start()

    forward(0)

    row_tiles = [(q_guest, pen_guest, 2, t, True) for t in range(tiles)]
    row_tiles += [(q_own, pen_own, 0, t, False) for t in range(tiles)]

    def one_head(h, carry):
        for copy in local_in(h):
            copy.wait()

        @pl.when(has_up)
        def _():
            q_copy(h).wait_recv()

        own_wide = with_ones(v_own[h])
        for n, (q_ref, pen_ref, first, t, _) in enumerate(row_tiles):
            at = pl.ds(n * tile, tile)
            s = scores_of(q_ref[h, pl.ds(t * tile, tile), :], k_own[h])
            penalty = pen_ref[first:first + 1, 0:1]
            top = jnp.maximum(jnp.max(s, axis=1, keepdims=True) - penalty, LOW)
            weights = jnp.exp2(s - (top + penalty)).astype(bf16)
            acc_ref[at, :] = jnp.dot(weights, own_wide, preferred_element_type=f32)
            top_ref[at, :] = top

        @pl.when(h >= 1)
        def _():
            for t in range(tiles):
                merge(h - 1, t)

        @pl.when(has_prev)
        def _():
            k_copy(h).wait_recv()

        @pl.when(h + 1 < heads)
        def _():
            forward(h + 1)

        for n, (q_ref, pen_ref, first, t, _) in enumerate(row_tiles):
            at = pl.ds(n * tile, tile)
            s = scores_of(q_ref[h, pl.ds(t * tile, tile), :], k_prev[h])
            penalty = pen_ref[first + 1:first + 2, 0:1]
            before = top_ref[at, :]
            top = jnp.maximum(jnp.max(s, axis=1, keepdims=True) - penalty, before)
            p_ref[at, :] = jnp.exp2(s - (top + penalty)).astype(bf16)
            acc_ref[at, :] = acc_ref[at, :] * jnp.exp2(before - top)
            top_ref[at, :] = top

        @pl.when(has_prev)
        def _():
            v_copy(h).wait_recv()

        prev_wide = with_ones(v_prev[h])
        for n, (_, _, _, t, guest) in enumerate(row_tiles):
            at = pl.ds(n * tile, tile)
            acc = acc_ref[at, :] + jnp.dot(p_ref[at, :], prev_wide, preferred_element_type=f32)
            total = jnp.maximum(acc[:, HD:], 1.0)
            out = acc[:, :HD] / total
            lse = top_ref[at, :] + jnp.log2(total)
            rows = pl.ds(t * tile, tile)
            if guest:
                o_send[h, rows, :] = out.astype(bf16)
                for a in range(tile // LANES):
                    st_send[h, t, a:a + 1, :] = jnp.sum(
                        jnp.where(eye, lse[a * LANES:(a + 1) * LANES, :], 0.0), axis=0, keepdims=True
                    )

                @pl.when(has_up)
                def _():
                    o_copy(h, t).start()
                    st_copy(h, t).start()
            else:
                o_loc[h, rows, :] = out
                lse_loc[h, rows, :] = lse
        return carry

    lax.fori_loop(0, heads, one_head, 0)

    w_in.wait()
    lat_in.wait()
    levels_in.wait()
    gate_in.wait()
    level = jnp.full((1, LANES), levels_ref[0], jnp.int32).astype(f32)
    delta = (noise_level(level / LEVELS) - noise_level((level + 1.0) / LEVELS))[:, 0:1]
    gate = jnp.zeros((1, out_width), f32)
    for n in range(LEVELS):
        gate = gate + jnp.where(level[:, 0:1] == float(n), gate_ref[n:n + 1, :], 0.0)
    gate_row[...] = gate

    def at_rows(i):
        return pl.ds(pl.multiple_of((i // col_parts) * prow, prow), prow)

    def at_cols(i, base=0):
        return pl.ds(pl.multiple_of(base + (i % col_parts) * pcol, LANES), pcol)

    def project(i, owner):
        return jnp.dot(
            attended[at_rows(i), :], w_ref[:, at_cols(i, owner * out_width)],
            preferred_element_type=f32,
        )

    def pair_copy(i):
        return remote(pair_send.at[i], pair_recv.at[i], pair_ss.at[i], pair_rs.at[i], head=pair)

    def near_copy(i):
        return remote(near_send.at[i], near_recv.at[i], near_ss.at[i], near_rs.at[i], head=pair)

    def far_copy(i):
        return remote(far_send.at[i], far_recv.at[i], far_ss.at[i], far_rs.at[i], head=far)

    def slide_copy(i):
        return remote(
            upd_stage.at[i], next_hbm.at[at_rows(i), at_cols(i)], slide_ss.at[i], slide_rs.at[i],
            frame=f - 1,
        )

    def vel_copy(i):
        return pltpu.make_async_copy(
            vel_stage.at[i], vel_hbm.at[at_rows(i), at_cols(i)], vel_sem.at[i]
        )

    diagonal = (pair + 2) % 4

    def send_pair(i):
        pair_send[i] = project(i, diagonal).astype(bf16)
        pair_copy(i).start()

    merge(heads - 1, 0)
    send_pair(0)

    def exchange(i, carry):
        for t in range(1, row_parts):
            @pl.when(i == t * col_parts - 2)
            def _():
                merge(heads - 1, t)

        @pl.when(i + 1 < pieces)
        def _():
            send_pair(i + 1)

        @pl.when(i < pieces)
        def _():
            mine = project(i, far)
            pair_copy(i).wait_recv()
            far_send[i] = (mine.astype(bf16).astype(f32) + pair_recv[i].astype(f32)).astype(bf16)
            far_copy(i).start()
            near_send[i] = project(i, pair).astype(bf16)
            near_copy(i).start()

        @pl.when(i >= lag)
        def _():
            join(i - lag)
        return carry

    def join(i):
        total = project(i, me).astype(bf16).astype(f32)
        near_copy(i).wait_recv()
        far_copy(i).wait_recv()
        total = total + near_recv[i].astype(f32) + far_recv[i].astype(f32)
        gated = gate_row[0:1, at_cols(i)] * total
        upd_stage[i] = (lat_ref[at_rows(i), at_cols(i)].astype(f32) + delta * gated).astype(bf16)

        @pl.when(has_prev)
        def _():
            slide_copy(i).start()
        vel_stage[i] = gated.astype(bf16)
        vel_copy(i).start()

    lax.fori_loop(0, pieces + lag, exchange, 0)

    for h in range(heads):
        @pl.when(has_next)
        def _():
            k_copy(h).wait_send()

        @pl.when(even & has_next)
        def _():
            v_copy(h).wait_send()

        @pl.when(has_down)
        def _():
            q_copy(h).wait_send()

        @pl.when(has_up)
        def _():
            for t in range(tiles):
                o_copy(h, t).wait_send()
                st_copy(h, t).wait_send()

    @pl.when(odd & has_next)
    def _():
        for h in range(1, heads):
            relay_in(h).wait_send()

    @pl.when(even & has_up)
    def _():
        for h in range(heads):
            relay_out(h).wait_send()

    @pl.when(has_down)
    def _():
        pen_copy.wait_send()

    @pl.when(f == frames - 1)
    def _():
        fresh_in = pltpu.make_async_copy(fresh_hbm, lat_ref, bulk_sem.at[0])
        fresh_in.start()
        fresh_in.wait()
        fresh_out = pltpu.make_async_copy(lat_ref, next_hbm, bulk_sem.at[1])
        fresh_out.start()
        fresh_out.wait()

    def drain(i, carry):
        pair_copy(i).wait_send()
        near_copy(i).wait_send()
        far_copy(i).wait_send()
        vel_copy(i).wait()

        @pl.when(has_prev)
        def _():
            slide_copy(i).wait_send()

        @pl.when(has_next)
        def _():
            slide_copy(i).wait_recv()
        return carry

    lax.fori_loop(0, pieces, drain, 0)


def shards(latents, queries, keys, values, out_weight, gate_table, levels, block_mask, fresh):
    span, hh = queries.shape
    heads = hh // HD
    out_width = latents.shape[1]
    assert lax.axis_size("head") == 4 and block_mask.shape[1] == 4
    assert out_weight.shape[1] == 4 * out_width
    prow = span // 2
    pcol = 2 * LANES if out_width % (2 * LANES) == 0 else LANES
    pieces = (span // prow) * (out_width // pcol)

    vmem = pltpu.VMEM
    dma = pltpu.SemaphoreType.DMA
    tiles = span // prow
    head_block = vmem((heads, span, HD), bf16)
    head_wide = vmem((heads, span, HD), f32)
    stats = vmem((heads, tiles, 8, LANES), f32)
    piece = vmem((pieces, prow, pcol), bf16)
    any_spec = pl.BlockSpec(memory_space=pl.ANY)
    out = jax.ShapeDtypeStruct((span, out_width), bf16)
    return pl.pallas_call(
        kernel,
        in_specs=[any_spec] * 9,
        out_specs=[any_spec, any_spec],
        out_shape=[out, out],
        scratch_shapes=[pltpu.SMEM((1,), jnp.int32), pltpu.SMEM((1, 4), jnp.int32)]
        + [vmem(gate_table.shape, f32)]
        + [head_block] * 7
        + [vmem((8, LANES), f32)] * 2
        + [vmem((2 * span, 2 * HD), f32), vmem((2 * span, 1), f32), vmem((2 * span, span), bf16)]
        + [head_block, head_block, stats, stats, head_wide, head_wide]
        + [vmem((span, hh), bf16), vmem(out_weight.shape, bf16), vmem((span, out_width), bf16)]
        + [vmem((1, out_width), f32)]
        + [piece] * 8
        + [dma((heads, 3)), dma((5,)), dma((heads, 2)), dma((heads, 2))]
        + [dma((heads,))] * 4
        + [dma((heads, tiles))] * 4
        + [dma((2,))]
        + [dma((pieces,))] * 9,
        compiler_params=pltpu.CompilerParams(
            collective_id=0, has_side_effects=True, vmem_limit_bytes=VMEM_LIMIT
        ),
    )(
        levels, block_mask, queries, keys, values, out_weight, latents, fresh, gate_table
    )


def solution(mesh):
    in_specs = (
        P("frame", "head"),
        P("frame", "head"),
        P("frame", "head"),
        P("frame", "head"),
        P("head", None),
        P(None, "head"),
        P("frame"),
        P("frame", None),
        P(None, "head"),
    )
    out_specs = (P("frame", "head"), P("frame", "head"))
    return jax.shard_map(shards, mesh=mesh, in_specs=in_specs, out_specs=out_specs, check_vma=False)
```

time: 95.3 us -> 99.2 us (1.041)
  the two profiles are of different devices: /device:TPU:25 before, /device:TPU:23 now
where the time goes in v1:
time: 99.2 us; the launch traced here: 97.9 us
  Pallas kernels  93 us (94%)
  local copies, waits for them, and re-layouts  3.62 us (4%)
  between operations  1.3 us (1%)
    pallas_call x1, Pallas kernels, shards(): pl.pallas_call(kernel, in_specs=[any_spec] * 9, out_specs=[any_spec, any_...  93 us
    unnamed x4, local copies, waits for them, and re-layouts  3.62 us

profile of v1, /device:TPU:23, one launch (start us, length us, event | category | flops | bytes accessed | tf_op | source)
XLA Modules:
  0.0 97.9 jit_solution(10371907975441958865)
XLA Ops:
  1.3 93.0 %shard_map.104 = (bf16[512,1280]{1,0:T(8,128)(2,1)}, bf16[512,1280]{1,0:T(8,128)(2,1)}) custom-call(s32[1]{0:T(128)S(6)} %copy.13.levels_hbm, s32[1,4]{1,0:T(1,128)} %mask_hbm.1, bf16[512,640]{1,0:T(8,128)(2,1)} %q_hbm.1, bf16[512,640]{1,0:T(8,128)(2,1)} %k_hbm.1, bf16[512,640]{1,0:T(8,128)(2,1)} %v_hbm.1, bf16[640,5120]{1,0:T(8,128)(2,1)} %w_hbm.1, ...), custom_call_target="tpu_custom_call" | custom-call | tf_op jit(solution)/shard_map/pallas_call | solution.py:466
  94.3 0.0 copy-start
  94.3 2.6 %copy.14 = bf16[512,1280]{1,0:T(8,128)(2,1)} copy(bf16[512,1280]{1,0:T(8,128)(2,1)} %get-tuple-element.4) | data formatting | bytes 2621440
  96.9 0.0 copy-done
  96.9 1.1 %copy.15 = bf16[512,1280]{1,0:T(8,128)(2,1)} copy(bf16[512,1280]{1,0:T(8,128)(2,1)S(1)} %copy-done) | data formatting | bytes 2621440
Async XLA Ops:
  94.3 2.6 %copy-start = (bf16[512,1280]{1,0:T(8,128)(2,1)S(1)}, bf16[512,1280]{1,0:T(8,128)(2,1)}, u32[]{:S(2)}) copy-start(bf16[512,1280]{1,0:T(8,128)(2,1)} %get-tuple-element.5) | copy-start | bytes 3932164

commit v2 on v1

--- a/solution.py
+++ b/solution.py
@@ -39,11 +39,11 @@
     levels_hbm, mask_hbm, q_hbm, k_hbm, v_hbm, w_hbm, lat_hbm, fresh_hbm, gate_hbm,
     vel_hbm, next_hbm,
     levels_ref, mask_ref, gate_ref,
-    q_own, k_own, v_own, q_guest, k_prev, v_prev, v_relay, pen_own, pen_guest,
+    q_own, k_own, v_own, q_guest, k_prev, v_prev, relay, pen_own, pen_guest,
     acc_ref, top_ref, p_ref,
     o_send, o_recv, st_send, st_recv, o_loc, lse_loc, attended, w_ref, lat_ref, gate_row,
     pair_send, pair_recv, near_send, near_recv, far_send, far_recv, vel_stage, upd_stage,
-    in_sem, bulk_sem, kv_ss, kv_rs, relay_ss, relay_rs, q_ss, q_rs, o_ss, o_rs, st_ss, st_rs, pen_sem,
+    in_sem, bulk_sem, kv_ss, kv_rs, relay_ss, relay_rs, fwd_ss, q_ss, q_rs, o_ss, o_rs, st_ss, st_rs, pen_sem,
     pair_ss, pair_rs, near_ss, near_rs, far_ss, far_rs, vel_sem, slide_ss, slide_rs,
 ):
     f = lax.axis_index("frame")
@@ -94,13 +94,21 @@
     def v_copy(h):
         return remote(v_hbm.at[:, columns(h)], v_prev.at[h], kv_ss.at[h, 1], kv_rs.at[h, 1], frame=f + 1)
 
-    def relay_in(h):
+    def relay_keys(h):
         return remote(
-            v_hbm.at[:, columns(h)], v_relay.at[h], relay_ss.at[h], relay_rs.at[h], frame=f - 1
-        )
-
-    def relay_out(h):
-        return remote(v_relay.at[h], v_prev.at[h], kv_ss.at[h, 1], kv_rs.at[h, 1], frame=f + 2)
+            k_hbm.at[:, columns(h)], relay.at[h], relay_ss.at[h, 0], relay_rs.at[h], frame=f - 1
+        )
+
+    def relay_values(h):
+        return remote(
+            v_hbm.at[:, columns(h)], relay.at[h], relay_ss.at[h, 1], relay_rs.at[h], frame=f + 2
+        )
+
+    def forward_keys(h):
+        return remote(relay.at[h], k_prev.at[h], fwd_ss.at[h], kv_rs.at[h, 0], frame=f + 2)
+
+    def forward_values(h):
+        return remote(relay.at[h], v_prev.at[h], fwd_ss.at[h], kv_rs.at[h, 1], frame=f - 1)
 
     def q_copy(h):
         return remote(q_hbm.at[:, columns(h)], q_guest.at[h], q_ss.at[h], q_rs.at[h], frame=f - 2)
@@ -143,6 +151,12 @@
     def _():
         q_guest[...] = jnp.zeros_like(q_guest)
         pen_guest[...] = jnp.zeros_like(pen_guest)
+
+    mask_in.wait()
+    for k in range(4):
+        allowed = (mask_ref[0, k] == 1) & (f - k >= 0)
+        pen_own[k:k + 1, :] = jnp.full((1, LANES), jnp.where(allowed, 0.0, FAR), f32)
+    pen_own[4:, :] = jnp.zeros((4, LANES), f32)
 
     others = (
         2 + has_prev.astype(jnp.int32) + has_down.astype(jnp.int32)
@@ -159,10 +173,13 @@
     @pl.when(odd & has_next)
     def _():
         for h in range(heads):
-            relay_in(h).start()
+            relay_values(h).start()
+        for h in range(2):
+            relay_keys(h).start()
 
     @pl.when(has_down)
     def _():
+        pen_copy.start()
         for h in range(heads):
             q_copy(h).start()
 
@@ -170,22 +187,6 @@
     levels_in.start()
     gate_in.start()
     lat_in.start()
-
-    mask_in.wait()
-    for k in range(4):
-        allowed = (mask_ref[0, k] == 1) & (f - k >= 0)
-        pen_own[k:k + 1, :] = jnp.full((1, LANES), jnp.where(allowed, 0.0, FAR), f32)
-    pen_own[4:, :] = jnp.zeros((4, LANES), f32)
-
-    @pl.when(has_down)
-    def _():
-        pen_copy.start()
-
-    @pl.when(odd & has_next)
-    def _():
-        relay_in(0).wait_send()
-        for h in range(heads):
-            k_copy(h).start()
 
     eye = lax.broadcasted_iota(jnp.int32, (LANES, LANES), 0) == lax.broadcasted_iota(
         jnp.int32, (LANES, LANES), 1
@@ -213,8 +214,17 @@
     def forward(h):
         @pl.when(even & has_up)
         def _():
-            relay_in(h).wait_recv()
-            relay_out(h).start()
+            relay_keys(h).wait_recv()
+            forward_keys(h).start()
+
+        @pl.when(odd & has_down)
+        def _():
+            relay_values(h).wait_recv()
+            forward_values(h).start()
+
+        @pl.when(odd & has_next & (h + 2 < heads))
+        def _():
+            relay_keys(h + 2).start()
 
     forward(0)
 
@@ -239,18 +249,13 @@
             acc_ref[at, :] = jnp.dot(weights, own_wide, preferred_element_type=f32)
             top_ref[at, :] = top
 
-        @pl.when(h >= 1)
-        def _():
-            for t in range(tiles):
-                merge(h - 1, t)
+        @pl.when(h + 1 < heads)
+        def _():
+            forward(h + 1)
 
         @pl.when(has_prev)
         def _():
             k_copy(h).wait_recv()
-
-        @pl.when(h + 1 < heads)
-        def _():
-            forward(h + 1)
 
         for n, (q_ref, pen_ref, first, t, _) in enumerate(row_tiles):
             at = pl.ds(n * tile, tile)
@@ -341,6 +346,12 @@
         pair_send[i] = project(i, diagonal).astype(bf16)
         pair_copy(i).start()
 
+    def merge_head(h, carry):
+        for t in range(tiles):
+            merge(h, t)
+        return carry
+
+    lax.fori_loop(0, heads - 1, merge_head, 0)
     merge(heads - 1, 0)
     send_pair(0)
 
@@ -385,12 +396,9 @@
     lax.fori_loop(0, pieces + lag, exchange, 0)
 
     for h in range(heads):
-        @pl.when(has_next)
+        @pl.when(even & has_next)
         def _():
             k_copy(h).wait_send()
-
-        @pl.when(even & has_next)
-        def _():
             v_copy(h).wait_send()
 
         @pl.when(has_down)
@@ -405,13 +413,14 @@
 
     @pl.when(odd & has_next)
     def _():
-        for h in range(1, heads):
-            relay_in(h).wait_send()
-
-    @pl.when(even & has_up)
-    def _():
         for h in range(heads):
-            relay_out(h).wait_send()
+            relay_keys(h).wait_send()
+            relay_values(h).wait_send()
+
+    @pl.when((even & has_up) | (odd & has_down))
+    def _():
+        for h in range(heads):
+            forward_keys(h).wait_send()
 
     @pl.when(has_down)
     def _():
@@ -449,7 +458,7 @@
     heads = hh // HD
     out_width = latents.shape[1]
     assert lax.axis_size("head") == 4 and block_mask.shape[1] == 4
-    assert out_weight.shape[1] == 4 * out_width
+    assert out_weight.shape[1] == 4 * out_width and lax.axis_size("frame") % 2 == 0
     prow = span // 2
     pcol = 2 * LANES if out_width % (2 * LANES) == 0 else LANES
     pieces = (span // prow) * (out_width // pcol)
@@ -478,6 +487,7 @@
         + [vmem((1, out_width), f32)]
         + [piece] * 8
         + [dma((heads, 3)), dma((5,)), dma((heads, 2)), dma((heads, 2))]
+        + [dma((heads, 2))]
         + [dma((heads,))] * 4
         + [dma((heads, tiles))] * 4
         + [dma((2,))]

time: 99.2 us -> 82.3 us (0.83)
  Pallas kernels: 93 us -> 76.1 us
    pallas_call x1, Pallas kernels: 93 us -> 76.1 us  [shards(): pl.pallas_call(kernel, in_specs=[any_spec] * 9, out_specs=[any_spec, any_...]
where the time goes in v2:
time: 82.3 us; the launch traced here: 81.1 us
  Pallas kernels  76.1 us (92%)
  local copies, waits for them, and re-layouts  3.62 us (4%)
  between operations  1.3 us (2%)
    pallas_call x1, Pallas kernels, shards(): pl.pallas_call(kernel, in_specs=[any_spec] * 9, out_specs=[any_spec, any_...  76.1 us
    unnamed x4, local copies, waits for them, and re-layouts  3.62 us

profile of v2, /device:TPU:23, one launch (start us, length us, event | category | flops | bytes accessed | tf_op | source)
XLA Modules:
  0.0 81.1 jit_solution(16258810143112732231)
XLA Ops:
  1.3 76.1 %shard_map.104 = (bf16[512,1280]{1,0:T(8,128)(2,1)}, bf16[512,1280]{1,0:T(8,128)(2,1)}) custom-call(s32[1]{0:T(128)S(6)} %copy.13.levels_hbm, s32[1,4]{1,0:T(1,128)} %mask_hbm.1, bf16[512,640]{1,0:T(8,128)(2,1)} %q_hbm.1, bf16[512,640]{1,0:T(8,128)(2,1)} %k_hbm.1, bf16[512,640]{1,0:T(8,128)(2,1)} %v_hbm.1, bf16[640,5120]{1,0:T(8,128)(2,1)} %w_hbm.1, ...), custom_call_target="tpu_custom_call" | custom-call | tf_op jit(solution)/shard_map/pallas_call | solution.py:475
  77.4 0.0 copy-start
  77.4 2.6 %copy.14 = bf16[512,1280]{1,0:T(8,128)(2,1)} copy(bf16[512,1280]{1,0:T(8,128)(2,1)} %get-tuple-element.4) | data formatting | bytes 2621440
  80.0 0.0 copy-done
  80.0 1.1 %copy.15 = bf16[512,1280]{1,0:T(8,128)(2,1)} copy(bf16[512,1280]{1,0:T(8,128)(2,1)S(1)} %copy-done) | data formatting | bytes 2621440
Async XLA Ops:
  77.4 2.6 %copy-start = (bf16[512,1280]{1,0:T(8,128)(2,1)S(1)}, bf16[512,1280]{1,0:T(8,128)(2,1)}, u32[]{:S(2)}) copy-start(bf16[512,1280]{1,0:T(8,128)(2,1)} %get-tuple-element.5) | copy-start | bytes 3932164

commit v3 on v2

v3 whole, which is shorter than its diff:
```python
import functools
import math

import jax
import jax.numpy as jnp
from jax import lax
from jax.experimental import pallas as pl
from jax.experimental.pallas import tpu as pltpu
from jax.sharding import PartitionSpec as P

HD = 128
LANES = 128
LEVELS = 4
FAR = 1e30
LOW = -1e20
AHEAD = 3
LAG = 4
WIDE = 256
PIECE_ROWS = 256
PIECE_COLS = 128
VMEM_LIMIT = 60 * 1024 * 1024

flow_shift = 5.0

MESH = pl.DeviceIdType.MESH
bf16 = jnp.bfloat16
f32 = jnp.float32


def noise_level(point):
    return flow_shift * point / (1.0 + (flow_shift - 1.0) * point)


def scores_of(query, keys):
    scale = math.log2(math.e) / math.sqrt(HD)
    return lax.dot_general(query, keys, (((1,), (1,)), ((), ())), preferred_element_type=f32) * scale


def row_max(scores):
    top = jnp.max(scores, axis=1, keepdims=True)
    return jnp.broadcast_to(top, (scores.shape[0], LANES))


def across(stat, width):
    return jnp.concatenate([stat] * (width // LANES), axis=1)


def with_ones(values):
    return jnp.concatenate([values, jnp.ones((values.shape[0], LANES), bf16)], axis=1)


def kernel(
    levels_hbm, mask_hbm, q_hbm, k_hbm, v_hbm, w_hbm, lat_hbm, fresh_hbm, gate_hbm,
    vel_hbm, next_hbm,
    levels_ref, mask_ref, gate_ref,
    q_own, k_own, v_own, q_guest, k_prev, v_prev, relay, pen_own, pen_guest,
    acc_ref, top_ref, fade_ref, p_ref,
    o_send, o_recv, st_send, st_recv, o_loc, lse_loc, attended, w_ref, lat_ref, gate_row,
    pair_send, pair_recv, near_send, near_recv, far_send, far_recv, vel_stage, upd_stage,
    in_sem, bulk_sem, kv_ss, kv_rs, relay_ss, relay_rs, fwd_ss, q_ss, q_rs, o_ss, o_rs, st_ss, st_rs, pen_sem,
    pair_ss, pair_rs, near_ss, near_rs, far_ss, far_rs, vel_sem, slide_ss, slide_rs,
):
    f = lax.axis_index("frame")
    frames = lax.axis_size("frame")
    me = lax.axis_index("head")
    heads, span, _ = q_own.shape
    pieces, prow, pcol = pair_send.shape
    row_parts = span // prow
    col_parts = pieces // row_parts
    out_width = lat_ref.shape[1]
    tile = o_send.shape[1] // o_rs.shape[1]
    tiles = span // tile
    lag = min(LAG, pieces)

    pair = me + 1 - 2 * (me % 2)
    far = (me + 2) % 4
    odd = f % 2 == 1
    even = f % 2 == 0
    has_prev = f >= 1
    has_down = f >= 2
    has_next = f + 1 < frames
    has_up = f + 2 < frames

    def remote(src, dst, ss, rs, frame=None, head=None):
        where = {"frame": frame} if head is None else {"head": head}
        return pltpu.make_async_remote_copy(
            src_ref=src, dst_ref=dst, send_sem=ss, recv_sem=rs, device_id=where, device_id_type=MESH
        )

    def arrived(whole, sem):
        pltpu.make_async_copy(whole, whole, sem).wait()

    def columns(h):
        return pl.ds(pl.multiple_of(h * HD, HD), HD)

    def local_in(h):
        return [
            pltpu.make_async_copy(src.at[:, columns(h)], dst.at[h], in_sem.at[i])
            for i, (src, dst) in enumerate(((k_hbm, k_own), (q_hbm, q_own), (v_hbm, v_own)))
        ]

    w_in = pltpu.make_async_copy(w_hbm, w_ref, bulk_sem.at[0])
    lat_in = pltpu.make_async_copy(lat_hbm, lat_ref, bulk_sem.at[1])
    mask_in = pltpu.make_async_copy(mask_hbm, mask_ref, bulk_sem.at[2])
    levels_in = pltpu.make_async_copy(levels_hbm, levels_ref, bulk_sem.at[3])
    gate_in = pltpu.make_async_copy(gate_hbm, gate_ref, bulk_sem.at[4])

    def k_copy(h):
        return remote(k_own.at[h], k_prev.at[h], kv_ss.at[0], kv_rs.at[h, 0], frame=f + 1)

    def v_copy(h):
        return remote(v_own.at[h], v_prev.at[h], kv_ss.at[1], kv_rs.at[h, 1], frame=f + 1)

    def relay_keys(h):
        return remote(
            k_own.at[h], relay.at[h], relay_ss.at[0], relay_rs.at[h], frame=f - 1
        )

    def relay_values(h):
        return remote(
            v_own.at[h], relay.at[h], relay_ss.at[1], relay_rs.at[h], frame=f + 2
        )

    def forward_keys(h):
        return remote(relay.at[h], k_prev.at[h], fwd_ss, kv_rs.at[h, 0], frame=f + 2)

    def forward_values(h):
        return remote(relay.at[h], v_prev.at[h], fwd_ss, kv_rs.at[h, 1], frame=f - 1)

    def q_copy(h):
        return remote(q_own.at[h], q_guest.at[h], q_ss, q_rs.at[h], frame=f - 2)

    def o_copy(h, t):
        rows = pl.ds(t * tile, tile)
        return remote(
            o_send.at[h, rows], o_recv.at[h, rows], o_ss, o_rs.at[h, t], frame=f + 2
        )

    def st_copy(h, t):
        return remote(st_send.at[h, t], st_recv.at[h, t], st_ss, st_rs.at[h, t], frame=f + 2)

    pen_copy = remote(pen_own, pen_guest, pen_sem.at[0], pen_sem.at[1], frame=f - 2)

    barrier = pltpu.get_barrier_semaphore()
    for there, step in ((has_prev, -1), (has_down, -2), (has_next, 1), (has_up, 2)):
        @pl.when(there)
        def _():
            pl.semaphore_signal(barrier, inc=1, device_id={"frame": f + step}, device_id_type=MESH)
    for peer in (pair, far):
        pl.semaphore_signal(barrier, inc=1, device_id={"head": peer}, device_id_type=MESH)

    mask_in.start()
    for h in range(heads):
        for copy in local_in(h):
            copy.start()

    @pl.when(f == 0)
    def _():
        k_prev[...] = jnp.zeros_like(k_prev)
        v_prev[...] = jnp.zeros_like(v_prev)

    @pl.when(f < 2)
    def _():
        o_recv[...] = jnp.zeros_like(o_recv)
        st_recv[...] = jnp.full(st_recv.shape, LOW, f32)

    @pl.when(f + 2 >= frames)
    def _():
        q_guest[...] = jnp.zeros_like(q_guest)
        pen_guest[...] = jnp.zeros_like(pen_guest)

    mask_in.wait()
    for k in range(4):
        allowed = (mask_ref[0, k] == 1) & (f - k >= 0)
        pen_own[k:k + 1, :] = jnp.full((1, LANES), jnp.where(allowed, 0.0, FAR), f32)
    pen_own[4:, :] = jnp.zeros((4, LANES), f32)

    others = (
        2 + has_prev.astype(jnp.int32) + has_down.astype(jnp.int32)
        + has_next.astype(jnp.int32) + has_up.astype(jnp.int32)
    )
    pl.semaphore_wait(barrier, others)
    for i, whole in enumerate((k_own, q_own, v_own)):
        arrived(whole, in_sem.at[i])

    @pl.when(even & has_next)
    def _():
        for h in range(heads):
            k_copy(h).start()
            v_copy(h).start()

    @pl.when(odd & has_next)
    def _():
        for h in range(heads):
            relay_values(h).start()
        for h in range(AHEAD):
            relay_keys(h).start()

    @pl.when(has_down)
    def _():
        pen_copy.start()
        for h in range(heads):
            q_copy(h).start()

    w_in.start()
    levels_in.start()
    gate_in.start()
    lat_in.start()

    eye = lax.broadcasted_iota(jnp.int32, (LANES, LANES), 0) == lax.broadcasted_iota(
        jnp.int32, (LANES, LANES), 1
    )

    def merge(h, t):
        @pl.when(has_down)
        def _():
            o_copy(h, t).wait_recv()
            st_copy(h, t).wait_recv()
        for a in range(tile // LANES):
            rows = pl.ds(t * tile + a * LANES, LANES)
            guest_lse = jnp.sum(
                jnp.where(eye, st_recv[h, t, a:a + 1, :], 0.0), axis=1, keepdims=True
            )
            share = 1.0 / (1.0 + jnp.exp2(lse_loc[h, rows, :] - guest_lse))
            mine = o_loc[h, rows, :]
            both = mine + share * (o_recv[h, rows, :].astype(f32) - mine)
            attended[rows, columns(h)] = both.astype(bf16)

    @pl.when(has_up)
    def _():
        pen_copy.wait_recv()

    def forward(h):
        @pl.when(even & has_up)
        def _():
            relay_keys(h).wait_recv()
            forward_keys(h).start()

        @pl.when(odd & has_down)
        def _():
            relay_values(h).wait_recv()
            forward_values(h).start()

        @pl.when(odd & has_next & (h + AHEAD < heads))
        def _():
            relay_keys(h + AHEAD).start()

    levels_in.wait()
    gate_in.wait()
    level = jnp.full((1, LANES), levels_ref[0], jnp.int32).astype(f32)
    delta = (noise_level(level / LEVELS) - noise_level((level + 1.0) / LEVELS))[:, 0:1]
    gate = jnp.zeros((1, out_width), f32)
    for n in range(LEVELS):
        gate = gate + jnp.where(level[:, 0:1] == float(n), gate_ref[n:n + 1, :], 0.0)
    gate_row[...] = gate

    forward(0)

    wide = min(WIDE, span)
    row_tiles = [(q_guest, pen_guest, 2, t, True) for t in range(span // wide)]
    row_tiles += [(q_own, pen_own, 0, t, False) for t in range(span // wide)]

    def own_part(h):
        @pl.when(has_up)
        def _():
            q_copy(h).wait_recv()

        own_wide = with_ones(v_own[h])
        for n, (q_ref, pen_ref, first, t, _) in enumerate(row_tiles):
            at = pl.ds(n * wide, wide)
            s = scores_of(q_ref[h, pl.ds(t * wide, wide), :], k_own[h])
            penalty = pen_ref[first:first + 1, :]
            top = jnp.maximum(row_max(s) - penalty, LOW)
            weights = jnp.exp2(s - across(top + penalty, span)).astype(bf16)
            acc_ref[h % 2, at, :] = jnp.dot(weights, own_wide, preferred_element_type=f32)
            top_ref[h % 2, at, :] = top

    own_part(0)
    forward(1)

    def one_head(h, carry):
        @pl.when(has_prev)
        def _():
            k_copy(h).wait_recv()

        for n, (q_ref, pen_ref, first, t, _) in enumerate(row_tiles):
            at = pl.ds(n * wide, wide)
            s = scores_of(q_ref[h, pl.ds(t * wide, wide), :], k_prev[h])
            penalty = pen_ref[first + 1:first + 2, :]
            before = top_ref[h % 2, at, :]
            top = jnp.maximum(row_max(s) - penalty, before)
            p_ref[at, :] = jnp.exp2(s - across(top + penalty, span)).astype(bf16)
            fade_ref[at, :] = jnp.exp2(before - top)
            top_ref[h % 2, at, :] = top

        @pl.when(h + 2 < heads)
        def _():
            forward(h + 2)

        @pl.when(h + 1 < heads)
        def _():
            own_part(h + 1)

        @pl.when(has_prev)
        def _():
            v_copy(h).wait_recv()

        prev_wide = with_ones(v_prev[h])
        for n in range(2 * tiles):
            guest, t = n < tiles, n % tiles
            at = pl.ds(n * tile, tile)
            acc = acc_ref[h % 2, at, :] * across(fade_ref[at, :], 2 * HD)
            acc = acc + jnp.dot(p_ref[at, :], prev_wide, preferred_element_type=f32)
            total = jnp.maximum(acc[:, HD:], 1.0)
            out = acc[:, :HD] / total
            lse = top_ref[h % 2, at, :] + jnp.log2(total)
            rows = pl.ds(t * tile, tile)
            if guest:
                o_send[h, rows, :] = out.astype(bf16)
                for a in range(tile // LANES):
                    st_send[h, t, a:a + 1, :] = jnp.sum(
                        jnp.where(eye, lse[a * LANES:(a + 1) * LANES, :], 0.0), axis=0, keepdims=True
                    )

                @pl.when(has_up)
                def _():
                    st_copy(h, t).start()
                    o_copy(h, t).start()
            else:
                o_loc[h, rows, :] = out
                lse_loc[h, rows, :] = lse

        @pl.when(h >= 2)
        def _():
            for t in range(tiles):
                merge(h - 2, t)
        return carry

    lax.fori_loop(0, heads, one_head, 0)

    w_in.wait()
    lat_in.wait()

    def at_rows(i):
        return pl.ds(pl.multiple_of((i // col_parts) * prow, prow), prow)

    def at_cols(i, base=0):
        return pl.ds(pl.multiple_of(base + (i % col_parts) * pcol, LANES), pcol)

    def project(i, owner):
        return jnp.dot(
            attended[at_rows(i), :], w_ref[:, at_cols(i, owner * out_width)],
            preferred_element_type=f32,
        )

    def pair_copy(i):
        return remote(pair_send.at[i], pair_recv.at[i], pair_ss, pair_rs.at[i], head=pair)

    def near_copy(i):
        return remote(near_send.at[i], near_recv.at[i], near_ss, near_rs.at[i], head=pair)

    def far_copy(i):
        return remote(far_send.at[i], far_recv.at[i], far_ss, far_rs.at[i], head=far)

    def slide_copy(i):
        return remote(
            upd_stage.at[i], next_hbm.at[at_rows(i), at_cols(i)], slide_ss, slide_rs,
            frame=f - 1,
        )

    def vel_copy(i):
        return pltpu.make_async_copy(
            vel_stage.at[i], vel_hbm.at[at_rows(i), at_cols(i)], vel_sem
        )

    diagonal = (pair + 2) % 4

    def send_pair(i):
        pair_send[i] = project(i, diagonal).astype(bf16)
        pair_copy(i).start()

    for t in range(tiles):
        merge(heads - 2, t)
    merge(heads - 1, 0)
    send_pair(0)

    def exchange(i, carry):
        for t in range(1, tiles):
            @pl.when(i == t * (pieces // tiles) - 2)
            def _():
                merge(heads - 1, t)

        @pl.when(i + 1 < pieces)
        def _():
            send_pair(i + 1)

        @pl.when(i < pieces)
        def _():
            mine = project(i, far)
            pair_copy(i).wait_recv()
            far_send[i] = (mine.astype(bf16).astype(f32) + pair_recv[i].astype(f32)).astype(bf16)
            far_copy(i).start()
            near_send[i] = project(i, pair).astype(bf16)
            near_copy(i).start()

        @pl.when(i >= lag)
        def _():
            join(i - lag)
        return carry

    def join(i):
        total = project(i, me).astype(bf16).astype(f32)
        near_copy(i).wait_recv()
        far_copy(i).wait_recv()
        total = total + near_recv[i].astype(f32) + far_recv[i].astype(f32)
        gated = gate_row[0:1, at_cols(i)] * total
        upd_stage[i] = (lat_ref[at_rows(i), at_cols(i)].astype(f32) + delta * gated).astype(bf16)

        @pl.when(has_prev)
        def _():
            slide_copy(i).start()
        vel_stage[i] = gated.astype(bf16)
        vel_copy(i).start()

    lax.fori_loop(0, pieces + lag, exchange, 0)

    @pl.when(even & has_next)
    def _():
        arrived(k_own, kv_ss.at[0])
        arrived(v_own, kv_ss.at[1])

    @pl.when(odd & has_next)
    def _():
        arrived(k_own, relay_ss.at[0])
        arrived(v_own, relay_ss.at[1])

    @pl.when((even & has_up) | (odd & has_down))
    def _():
        arrived(relay, fwd_ss)

    @pl.when(has_up)
    def _():
        arrived(o_send, o_ss)
        arrived(st_send, st_ss)

    @pl.when(has_down)
    def _():
        arrived(q_own, q_ss)

    @pl.when(has_down)
    def _():
        pen_copy.wait_send()

    @pl.when(f == frames - 1)
    def _():
        fresh_in = pltpu.make_async_copy(fresh_hbm, lat_ref, bulk_sem.at[0])
        fresh_in.start()
        fresh_in.wait()
        fresh_out = pltpu.make_async_copy(lat_ref, next_hbm, bulk_sem.at[1])
        fresh_out.start()
        fresh_out.wait()

    arrived(pair_send, pair_ss)
    arrived(near_send, near_ss)
    arrived(far_send, far_ss)
    arrived(vel_stage, vel_sem)

    @pl.when(has_prev)
    def _():
        arrived(upd_stage, slide_ss)

    @pl.when(has_next)
    def _():
        arrived(upd_stage, slide_rs)


def shards(latents, queries, keys, values, out_weight, gate_table, levels, block_mask, fresh):
    span, hh = queries.shape
    heads = hh // HD
    out_width = latents.shape[1]
    assert lax.axis_size("head") == 4 and block_mask.shape[1] == 4
    assert out_weight.shape[1] == 4 * out_width and lax.axis_size("frame") % 2 == 0
    tiles = 2
    prow, pcol = min(PIECE_ROWS, span // tiles), PIECE_COLS
    assert span % (tiles * prow) == 0 and out_width % pcol == 0
    pieces = (span // prow) * (out_width // pcol)

    vmem = pltpu.VMEM
    dma = pltpu.SemaphoreType.DMA
    head_block = vmem((heads, span, HD), bf16)
    head_wide = vmem((heads, span, HD), f32)
    stats = vmem((heads, tiles, 8, LANES), f32)
    piece = vmem((pieces, prow, pcol), bf16)
    any_spec = pl.BlockSpec(memory_space=pl.ANY)
    out = jax.ShapeDtypeStruct((span, out_width), bf16)
    return pl.pallas_call(
        kernel,
        in_specs=[any_spec] * 9,
        out_specs=[any_spec, any_spec],
        out_shape=[out, out],
        scratch_shapes=[pltpu.SMEM((1,), jnp.int32), pltpu.SMEM((1, 4), jnp.int32)]
        + [vmem(gate_table.shape, f32)]
        + [head_block] * 7
        + [vmem((8, LANES), f32)] * 2
        + [vmem((2, 2 * span, 2 * HD), f32), vmem((2, 2 * span, LANES), f32)]
        + [vmem((2 * span, LANES), f32), vmem((2 * span, span), bf16)]
        + [head_block, head_block, stats, stats, head_wide, head_wide]
        + [vmem((span, hh), bf16), vmem(out_weight.shape, bf16), vmem((span, out_width), bf16)]
        + [vmem((1, out_width), f32)]
        + [piece] * 8
        + [dma((3,)), dma((5,)), dma((2,)), dma((heads, 2)), dma((2,)), dma((heads,)), dma(())]
        + [dma(()), dma((heads,))]
        + [dma(()), dma((heads, tiles))] * 2
        + [dma((2,))]
        + [dma(()), dma((pieces,))] * 3
        + [dma(())] * 3,
        compiler_params=pltpu.CompilerParams(
            collective_id=0, has_side_effects=True, vmem_limit_bytes=VMEM_LIMIT
        ),
    )(
        levels, block_mask, queries, keys, values, out_weight, latents, fresh, gate_table
    )


def solution(mesh):
    in_specs = (
        P("frame", "head"),
        P("frame", "head"),
        P("frame", "head"),
        P("frame", "head"),
        P("head", None),
        P(None, "head"),
        P("frame"),
        P("frame", None),
        P(None, "head"),
    )
    out_specs = (P("frame", "head"), P("frame", "head"))
    return jax.shard_map(shards, mesh=mesh, in_specs=in_specs, out_specs=out_specs, check_vma=False)
```

time: 82.3 us -> 78.9 us (0.959); the launches traced: 81.1 us -> 78.7 us
  Pallas kernels: 76.1 us -> 73.8 us
    pallas_call x1, Pallas kernels: 76.1 us -> 73.8 us  [shards(): pl.pallas_call(kernel, in_specs=[any_spec] * 9, out_specs=[any_spec, any_...]
where the time goes in v3:
time: 78.9 us; the launch traced here: 78.7 us
  Pallas kernels  73.8 us (94%)
  local copies, waits for them, and re-layouts  3.62 us (5%)
  between operations  1.3 us (2%)
    pallas_call x1, Pallas kernels, shards(): pl.pallas_call(kernel, in_specs=[any_spec] * 9, out_specs=[any_spec, any_...  73.8 us
    unnamed x4, local copies, waits for them, and re-layouts  3.62 us

profile of v3, /device:TPU:23, one launch (start us, length us, event | category | flops | bytes accessed | tf_op | source)
XLA Modules:
  0.0 78.7 jit_solution(6312879006977916928)
XLA Ops:
  1.3 73.8 %shard_map.104 = (bf16[512,1280]{1,0:T(8,128)(2,1)}, bf16[512,1280]{1,0:T(8,128)(2,1)}) custom-call(s32[1]{0:T(128)S(6)} %copy.13.levels_hbm, s32[1,4]{1,0:T(1,128)} %mask_hbm.1, bf16[512,640]{1,0:T(8,128)(2,1)} %q_hbm.1, bf16[512,640]{1,0:T(8,128)(2,1)} %k_hbm.1, bf16[512,640]{1,0:T(8,128)(2,1)} %v_hbm.1, bf16[640,5120]{1,0:T(8,128)(2,1)} %w_hbm.1, ...), custom_call_target="tpu_custom_call" | custom-call | tf_op jit(solution)/shard_map/pallas_call | solution.py:496
  75.1 0.0 copy-start
  75.1 2.6 %copy.14 = bf16[512,1280]{1,0:T(8,128)(2,1)} copy(bf16[512,1280]{1,0:T(8,128)(2,1)} %get-tuple-element.4) | data formatting | bytes 2621440
  77.7 0.0 copy-done
  77.7 1.1 %copy.15 = bf16[512,1280]{1,0:T(8,128)(2,1)} copy(bf16[512,1280]{1,0:T(8,128)(2,1)S(1)} %copy-done) | data formatting | bytes 2621440
Async XLA Ops:
  75.1 2.6 %copy-start = (bf16[512,1280]{1,0:T(8,128)(2,1)S(1)}, bf16[512,1280]{1,0:T(8,128)(2,1)}, u32[]{:S(2)}) copy-start(bf16[512,1280]{1,0:T(8,128)(2,1)} %get-tuple-element.5) | copy-start | bytes 3932164

commit v4 on v3

--- a/solution.py
+++ b/solution.py
@@ -192,9 +192,9 @@
     @pl.when(odd & has_next)
     def _():
         for h in range(heads):
+            if h < AHEAD:
+                relay_keys(h).start()
             relay_values(h).start()
-        for h in range(AHEAD):
-            relay_keys(h).start()
 
     @pl.when(has_down)
     def _():
@@ -474,6 +474,42 @@
         arrived(upd_stage, slide_rs)
 
 
+def settle_kernel(a_hbm, b_hbm, a_out, b_out, stage, in_sem, out_sem):
+    count, rows, _ = stage.shape
+    half = count // 2
+    ins, outs = [], []
+    for i in range(count):
+        src, dst = (a_hbm, a_out) if i < half else (b_hbm, b_out)
+        at = pl.ds((i % half) * rows, rows)
+        ins.append(pltpu.make_async_copy(src.at[at], stage.at[i], in_sem.at[i]))
+        outs.append(pltpu.make_async_copy(stage.at[i], dst.at[at], out_sem.at[i]))
+        ins[-1].start()
+    for copy_in, copy_out in zip(ins, outs):
+        copy_in.wait()
+        copy_out.start()
+    for copy_out in outs:
+        copy_out.wait()
+
+
+def settle(a, b):
+    count = 8
+    rows, width = a.shape
+    any_spec = pl.BlockSpec(memory_space=pl.ANY)
+    out = jax.ShapeDtypeStruct(a.shape, a.dtype)
+    return pl.pallas_call(
+        settle_kernel,
+        in_specs=[any_spec] * 2,
+        out_specs=[any_spec] * 2,
+        out_shape=[out, out],
+        scratch_shapes=[
+            pltpu.VMEM((count, 2 * rows // count, width), a.dtype),
+            pltpu.SemaphoreType.DMA((count,)),
+            pltpu.SemaphoreType.DMA((count,)),
+        ],
+        compiler_params=pltpu.CompilerParams(vmem_limit_bytes=VMEM_LIMIT),
+    )(a, b)
+
+
 def shards(latents, queries, keys, values, out_weight, gate_table, levels, block_mask, fresh):
     span, hh = queries.shape
     heads = hh // HD
@@ -493,7 +529,7 @@
     piece = vmem((pieces, prow, pcol), bf16)
     any_spec = pl.BlockSpec(memory_space=pl.ANY)
     out = jax.ShapeDtypeStruct((span, out_width), bf16)
-    return pl.pallas_call(
+    velocity, next_latents = pl.pallas_call(
         kernel,
         in_specs=[any_spec] * 9,
         out_specs=[any_spec, any_spec],
@@ -520,6 +556,7 @@
     )(
         levels, block_mask, queries, keys, values, out_weight, latents, fresh, gate_table
     )
+    return settle(velocity, next_latents)
 
 
 def solution(mesh):

time: 78.9 us -> 77.9 us (0.987)
  local copies, waits for them, and re-layouts: 3.62 us -> 0 us
  Pallas kernels: 73.8 us -> 76.4 us
    unnamed x4 -> x0, local copies, waits for them, and re-layouts: 3.62 us -> none
    pallas_call x0 -> x1, Pallas kernels: none -> 2.59 us  [settle(): pl.pallas_call(settle_kernel, in_specs=[any_spec] * 2, out_specs=[any_spe...]
where the time goes in v4:
time: 77.9 us; the launch traced here: 77.7 us
  Pallas kernels  76.4 us (98%)
  between operations  1.29 us (2%)
    pallas_call x1, Pallas kernels, shards(): pl.pallas_call(kernel, in_specs=[any_spec] * 9, out_specs=[any_spec, any_...  73.8 us
    pallas_call x1, Pallas kernels, settle(): pl.pallas_call(settle_kernel, in_specs=[any_spec] * 2, out_specs=[any_spe...  2.59 us

profile of v4, /device:TPU:23, one launch (start us, length us, event | category | flops | bytes accessed | tf_op | source)
XLA Modules:
  0.0 77.7 jit_solution(18109622526957666402)
XLA Ops:
  1.3 73.8 %shard_map.104 = (bf16[512,1280]{1,0:T(8,128)(2,1)}, bf16[512,1280]{1,0:T(8,128)(2,1)}) custom-call(s32[1]{0:T(128)S(6)} %copy.11.levels_hbm, s32[1,4]{1,0:T(1,128)} %mask_hbm.1, bf16[512,640]{1,0:T(8,128)(2,1)} %q_hbm.1, bf16[512,640]{1,0:T(8,128)(2,1)} %k_hbm.1, bf16[512,640]{1,0:T(8,128)(2,1)} %v_hbm.1, bf16[640,5120]{1,0:T(8,128)(2,1)} %w_hbm.1, ...), custom_call_target="tpu_custom_call" | custom-call | tf_op jit(solution)/shard_map/pallas_call | solution.py:532
  75.1 2.6 %shard_map.105 = (bf16[512,1280]{1,0:T(8,128)(2,1)}, bf16[512,1280]{1,0:T(8,128)(2,1)}) custom-call(bf16[512,1280]{1,0:T(8,128)(2,1)} %get-tuple-element.4.a_hbm, bf16[512,1280]{1,0:T(8,128)(2,1)} %get-tuple-element.5.b_hbm), custom_call_target="tpu_custom_call" | custom-call | tf_op jit(solution)/shard_map/pallas_call | solution.py:499

commit v5 on v4

--- a/solution.py
+++ b/solution.py
@@ -322,10 +322,22 @@
                         jnp.where(eye, lse[a * LANES:(a + 1) * LANES, :], 0.0), axis=0, keepdims=True
                     )
 
-                @pl.when(has_up)
-                def _():
-                    st_copy(h, t).start()
-                    o_copy(h, t).start()
+                if t == 0:
+                    @pl.when(has_up)
+                    def _():
+                        st_copy(h, 0).start()
+                        o_copy(h, 0).start()
+                else:
+                    @pl.when(has_up & (h < heads - 2))
+                    def _():
+                        st_copy(h, t).start()
+                        o_copy(h, t).start()
+
+                    @pl.when(has_up & (h == heads - 1))
+                    def _():
+                        for late in range(max(heads - 2, 0), heads):
+                            st_copy(late, t).start()
+                            o_copy(late, t).start()
             else:
                 o_loc[h, rows, :] = out
                 lse_loc[h, rows, :] = lse
@@ -379,16 +391,16 @@
         pair_send[i] = project(i, diagonal).astype(bf16)
         pair_copy(i).start()
 
-    for t in range(tiles):
-        merge(heads - 2, t)
-    merge(heads - 1, 0)
+    for h in range(max(heads - 2, 0), heads):
+        merge(h, 0)
     send_pair(0)
 
     def exchange(i, carry):
         for t in range(1, tiles):
             @pl.when(i == t * (pieces // tiles) - 2)
             def _():
-                merge(heads - 1, t)
+                for h in range(max(heads - 2, 0), heads):
+                    merge(h, t)
 
         @pl.when(i + 1 < pieces)
         def _():

time: 77.9 us -> 77.1 us (0.990)
  Pallas kernels: 76.4 us -> 75.6 us
    pallas_call x1, Pallas kernels: 73.8 us -> 73 us  [shards(): pl.pallas_call(kernel, in_specs=[any_spec] * 9, out_specs=[any_spec, any_...]
where the time goes in v5:
time: 77.1 us; the launch traced here: 76.9 us
  Pallas kernels  75.6 us (98%)
  between operations  1.29 us (2%)
    pallas_call x1, Pallas kernels, shards(): pl.pallas_call(kernel, in_specs=[any_spec] * 9, out_specs=[any_spec, any_...  73 us
    pallas_call x1, Pallas kernels, settle(): pl.pallas_call(settle_kernel, in_specs=[any_spec] * 2, out_specs=[any_spe...  2.59 us

profile of v5, /device:TPU:23, one launch (start us, length us, event | category | flops | bytes accessed | tf_op | source)
XLA Modules:
  0.0 76.9 jit_solution(16696199407064933018)
XLA Ops:
  1.3 73.0 %shard_map.104 = (bf16[512,1280]{1,0:T(8,128)(2,1)}, bf16[512,1280]{1,0:T(8,128)(2,1)}) custom-call(s32[1]{0:T(128)S(6)} %copy.11.levels_hbm, s32[1,4]{1,0:T(1,128)} %mask_hbm.1, bf16[512,640]{1,0:T(8,128)(2,1)} %q_hbm.1, bf16[512,640]{1,0:T(8,128)(2,1)} %k_hbm.1, bf16[512,640]{1,0:T(8,128)(2,1)} %v_hbm.1, bf16[640,5120]{1,0:T(8,128)(2,1)} %w_hbm.1, ...), custom_call_target="tpu_custom_call" | custom-call | tf_op jit(solution)/shard_map/pallas_call | solution.py:544
  74.3 2.6 %shard_map.105 = (bf16[512,1280]{1,0:T(8,128)(2,1)}, bf16[512,1280]{1,0:T(8,128)(2,1)}) custom-call(bf16[512,1280]{1,0:T(8,128)(2,1)} %get-tuple-element.4.a_hbm, bf16[512,1280]{1,0:T(8,128)(2,1)} %get-tuple-element.5.b_hbm), custom_call_target="tpu_custom_call" | custom-call | tf_op jit(solution)/shard_map/pallas_call | solution.py:511

commit v6 on v5

--- a/solution.py
+++ b/solution.py
@@ -106,19 +106,19 @@
     gate_in = pltpu.make_async_copy(gate_hbm, gate_ref, bulk_sem.at[4])
 
     def k_copy(h):
-        return remote(k_own.at[h], k_prev.at[h], kv_ss.at[0], kv_rs.at[h, 0], frame=f + 1)
+        return remote(k_hbm.at[:, columns(h)], k_prev.at[h], kv_ss.at[0], kv_rs.at[h, 0], frame=f + 1)
 
     def v_copy(h):
-        return remote(v_own.at[h], v_prev.at[h], kv_ss.at[1], kv_rs.at[h, 1], frame=f + 1)
+        return remote(v_hbm.at[:, columns(h)], v_prev.at[h], kv_ss.at[1], kv_rs.at[h, 1], frame=f + 1)
 
     def relay_keys(h):
         return remote(
-            k_own.at[h], relay.at[h], relay_ss.at[0], relay_rs.at[h], frame=f - 1
+            k_hbm.at[:, columns(h)], relay.at[h], relay_ss.at[0], relay_rs.at[h], frame=f - 1
         )
 
     def relay_values(h):
         return remote(
-            v_own.at[h], relay.at[h], relay_ss.at[1], relay_rs.at[h], frame=f + 2
+            v_hbm.at[:, columns(h)], relay.at[h], relay_ss.at[1], relay_rs.at[h], frame=f + 2
         )
 
     def forward_keys(h):
@@ -128,7 +128,7 @@
         return remote(relay.at[h], v_prev.at[h], fwd_ss, kv_rs.at[h, 1], frame=f - 1)
 
     def q_copy(h):
-        return remote(q_own.at[h], q_guest.at[h], q_ss, q_rs.at[h], frame=f - 2)
+        return remote(q_hbm.at[:, columns(h)], q_guest.at[h], q_ss, q_rs.at[h], frame=f - 2)
 
     def o_copy(h, t):
         rows = pl.ds(t * tile, tile)
@@ -180,9 +180,6 @@
         + has_next.astype(jnp.int32) + has_up.astype(jnp.int32)
     )
     pl.semaphore_wait(barrier, others)
-    for i, whole in enumerate((k_own, q_own, v_own)):
-        arrived(whole, in_sem.at[i])
-
     @pl.when(even & has_next)
     def _():
         for h in range(heads):
@@ -274,6 +271,9 @@
             weights = jnp.exp2(s - across(top + penalty, span)).astype(bf16)
             acc_ref[h % 2, at, :] = jnp.dot(weights, own_wide, preferred_element_type=f32)
             top_ref[h % 2, at, :] = top
+
+    for i, whole in enumerate((k_own, q_own, v_own)):
+        arrived(whole, in_sem.at[i])
 
     own_part(0)
     forward(1)

time: 77.1 us -> 77.1 us (level)
  no operation moved by 1% of the time
where the time goes in v6:
time: 77.1 us; the launch traced here: 77 us
  Pallas kernels  75.7 us (98%)
  between operations  1.29 us (2%)
    pallas_call x1, Pallas kernels, shards(): pl.pallas_call(kernel, in_specs=[any_spec] * 9, out_specs=[any_spec, any_...  73.1 us
    pallas_call x1, Pallas kernels, settle(): pl.pallas_call(settle_kernel, in_specs=[any_spec] * 2, out_specs=[any_spe...  2.59 us

profile of v6, /device:TPU:23, one launch (start us, length us, event | category | flops | bytes accessed | tf_op | source)
XLA Modules:
  0.0 77.0 jit_solution(285817432705092470)
XLA Ops:
  1.3 73.1 %shard_map.104 = (bf16[512,1280]{1,0:T(8,128)(2,1)}, bf16[512,1280]{1,0:T(8,128)(2,1)}) custom-call(s32[1]{0:T(128)S(6)} %copy.11.levels_hbm, s32[1,4]{1,0:T(1,128)} %mask_hbm.1, bf16[512,640]{1,0:T(8,128)(2,1)} %q_hbm.1, bf16[512,640]{1,0:T(8,128)(2,1)} %k_hbm.1, bf16[512,640]{1,0:T(8,128)(2,1)} %v_hbm.1, bf16[640,5120]{1,0:T(8,128)(2,1)} %w_hbm.1, ...), custom_call_target="tpu_custom_call" | custom-call | tf_op jit(solution)/shard_map/pallas_call | solution.py:544
  74.4 2.6 %shard_map.105 = (bf16[512,1280]{1,0:T(8,128)(2,1)}, bf16[512,1280]{1,0:T(8,128)(2,1)}) custom-call(bf16[512,1280]{1,0:T(8,128)(2,1)} %get-tuple-element.4.a_hbm, bf16[512,1280]{1,0:T(8,128)(2,1)} %get-tuple-element.5.b_hbm), custom_call_target="tpu_custom_call" | custom-call | tf_op jit(solution)/shard_map/pallas_call | solution.py:511
